TPU v7x, 32 devices: a whole 2x2x4 slice. The times are simulated.
32 devices in a mesh: kpt: 2 (over x), grid: 16 (over z, y, core).
Axes of the slice: x: 2, y: 2, z: 4, core: 2. Of those that a mesh axis runs over, the one named last changes fastest.
Arguments:
- orbitals: bfloat16 [4, 2, 2, 512, 256, 256], P('kpt', None, None, 'grid'), may hold values from -6 to 6
- kweights: int32 [4], P('kpt'), may hold values from 1 to 16
- occupations: int32 [4, 2], P('kpt'), may hold values from 0 to 2
- z_basis: float32 [512, 512], replicated, may hold values from -0.25 to 0.25
- z_eigen: float32 [512], replicated, may hold values from 0.25 to 4
Outputs:
- potential: float32 [512, 256, 256], P('grid')
All inputs are finite; a program needn't handle non-finite values.
Results may differ from a plain program's by a relative error of at most 0.0003.
Values sent between devices are 32-bit elements; how exact they have to be, the bound alone decides.
No kernel may reach another device: no remote copies, remote signals or barrier semaphores. Data moves between devices by JAX's collectives and lax.ppermute only.
A program may use at most 128 MiB of HBM per device.

v0:
```python
from functools import partial
import jax
import jax.numpy as jnp
from jax import lax
from jax.sharding import PartitionSpec as P

precise = lax.Precision.HIGHEST


def real_basis(length):
    position = jnp.arange(length, dtype=jnp.int32)
    product = position[:, None] * position[None, :] % length
    angles = product.astype(jnp.float32) * (2.0 * jnp.pi / length)
    lower = position[:, None] <= length // 2
    table = jnp.where(lower, jnp.cos(angles), jnp.sin(angles))
    edges = (position == 0) | (position == length // 2)
    weights = jnp.where(edges, 1.0, 2.0).astype(jnp.float32) / length
    return (table, table * weights[:, None])


def forward_real(density, bases):
    table_x, scaled_x, table_y, scaled_y = bases
    along = jnp.einsum("zxy,ky->zxk", density, table_y, precision=precise)
    return jnp.einsum("jx,zxk->zjk", table_x, along, precision=precise)[None]


def inverse_real(planes, bases):
    table_x, scaled_x, table_y, scaled_y = bases
    half_done = jnp.einsum("jx,zjk->zxk", scaled_x, planes[0], precision=precise)
    return jnp.einsum("zxk,ky->zxy", half_done, scaled_y, precision=precise)


def scale_table(z_eigen, kx_start, kx_count, x_length, y_length):
    wave_x = (kx_start + jnp.arange(kx_count, dtype=jnp.int32)).astype(jnp.float32)
    wave_y = jnp.arange(y_length, dtype=jnp.int32).astype(jnp.float32)
    shift_x = 2.0 * jnp.sin(jnp.pi * wave_x / x_length)
    shift_y = 2.0 * jnp.sin(jnp.pi * wave_y / y_length)
    shifted = shift_x[:, None] ** 2 + shift_y[None, :] ** 2
    return 1.0 / (z_eigen[:, None, None] + shifted[None])


def kernel_columns(z_rows, factors, columns):
    projected = jnp.einsum("zj,czab->cjab", z_rows, columns, precision=precise)
    return jnp.einsum("zj,cjab->czab", z_rows, projected * factors[None], precision=precise)


def on_device(orbitals, kweights, occupations, z_basis, z_eigen):
    points = orbitals.shape[0]
    band_count = orbitals.shape[1]
    x_length = orbitals.shape[4]
    y_length = orbitals.shape[5]
    factor = (kweights[:, None] * occupations).astype(jnp.float32) / (16.0 * points * band_count)
    values = orbitals.astype(jnp.float32)
    partial_sum = jnp.sum(factor[:, :, None, None, None, None] * values * values, axis=(0, 1, 2))
    table_x, scaled_x = real_basis(x_length)
    table_y, scaled_y = real_basis(y_length)
    forward = partial(forward_real, bases=(table_x, scaled_x, table_y, scaled_y))
    inverse = partial(inverse_real, bases=(table_x, scaled_x, table_y, scaled_y))
    blocks = lax.axis_size("grid")
    density = lax.psum(partial_sum, "kpt")
    spectrum = forward(density)
    kx_count = x_length // blocks
    kx_start = lax.axis_index("grid") * kx_count
    factors = scale_table(z_eigen, kx_start, kx_count, x_length, y_length)
    columns = kernel_columns(
        z_basis, factors, lax.all_to_all(spectrum, "grid", split_axis=2, concat_axis=1, tiled=True)
    )
    planes = lax.all_to_all(columns, "grid", split_axis=1, concat_axis=2, tiled=True)
    potential = inverse(planes)
    return potential


def solution(mesh):
    return jax.shard_map(
        on_device,
        mesh=mesh,
        in_specs=(P("kpt", None, None, "grid", None, None), P("kpt"), P("kpt", None), P(), P()),
        out_specs=P("grid", None, None),
        check_vma=False,
    )
```

profile of v0, /device:TPU:13, one launch (start us, length us, event | category | flops | bytes accessed | tf_op | source)
XLA Modules:
  0.0 750.4 jit_solution(17960610065291599581)
XLA Ops:
  6.5 0.0 all-reduce.2.cloned.1.call-start
  6.5 0.8 convert_multiply_fusion
  7.4 18.9 %fusion = f32[32,256,256]{2,1,0:T(8,128)} fusion(bf16[2,2,2,32,256,256]{5,4,3,2,1,0:T(8,128)(2,1)} %param.5, f32[2,2]{1,0:T(2,128)S(1)} %convert_multiply_fusion), kind=kLoop, calls=%fused_computation.1 | loop fusion | flops 65011712 | bytes 41943056 | tf_op jit(solution)/shard_map/reduce_sum | solution.py:54
  26.3 0.0 all-reduce.2.cloned.1.call-update
  26.4 199.1 %all-reduce.2.cloned.1.call-done = f32[32,256,256]{2,1,0:T(8,128)} async-done(((f32[32,256,256]{2,1,0:T(8,128)}), f32[32,256,256]{2,1,0:T(8,128)}) %all-reduce.2.cloned.1.call-update) | async-done | bytes 8388624 | tf_op jit(solution)/shard_map/psum | solution.py:60
  225.5 12.7 %fusion.25 = f32[32,256,256]{1,2,0:T(8,128)S(1)} fusion(f32[32,256,256]{2,1,0:T(8,128)} %all-reduce.2.cloned.1.call-done, pred[256]{0:T(512)(128)(4,1)S(1)} %iota_compare_fusion), kind=kOutput, calls=%fused_computation.28 | convolution fusion | flops 6443433984 | bytes 16777472 | tf_op jit(solution)/shard_map/zxy,ky->zxk/dot_general | solution.py:23
  238.2 23.2 %convolution_bitcast_fusion = f32[1,32,256,256]{2,3,1,0:T(8,128)} fusion(f32[32,256,256]{1,2,0:T(8,128)S(1)} %fusion.25, pred[256]{0:T(512)(128)(4,1)S(1)} %iota_compare_fusion), kind=kOutput, calls=%fused_computation.14 | convolution fusion | flops 6443433984 | bytes 16777472 | tf_op jit(solution)/shard_map/jx,zxk->zjk/dot_general | solution.py:24
  261.4 10.3 %copy.13 = f32[1,32,256,256]{3,1,0,2:T(8,128)} copy(f32[1,32,256,256]{2,3,1,0:T(8,128)} %convolution_bitcast_fusion) | data formatting | bytes 16777216 | tf_op jit(solution)/shard_map/broadcast_in_dim | solution.py:24
  271.7 6.5 all-to-all-start
  278.3 0.1 broadcast_add_fusion
  278.4 182.2 %all-to-all-done = f32[1,32,256,256]{3,1,0,2:T(8,128)} async-done(((f32[1,32,256,256]{3,1,0,2:T(8,128)}), f32[1,32,256,256]{3,1,0,2:T(8,128)}, u32[]{:S(2)}, u32[]{:S(2)}) %all-to-all-start) | async-done | bytes 8388640 | tf_op jit(solution)/shard_map/all_to_all | solution.py:66
  460.6 8.2 %copy.14 = f32[1,32,256,256]{3,2,1,0:T(8,128)S(1)} copy(f32[1,32,256,256]{3,1,0,2:T(8,128)} %all-to-all-done) | data formatting | bytes 16777216 | tf_op jit(solution)/shard_map/all_to_all | solution.py:66
  468.8 1.4 copy.15
  470.2 0.0 copy-done
  470.2 0.0 copy-start.2
  470.2 21.4 %fusion.6 = f32[16,256,512]{2,1,0:T(8,128)S(1)} fusion(f32[512,16,256]{2,1,0:T(8,128)S(1)} %bitcast.51, f32[512,512]{1,0:T(8,128)S(1)} %copy-done), kind=kOutput, calls=%fused_computation.7 | convolution fusion | flops 12884901888 | bytes 17825792 | tf_op jit(solution)/shard_map/zj,czab->cjab/dot_general | solution.py:43
  491.7 16.4 %fusion.13 = f32[1,512,16,256]{1,3,2,0:T(8,128)} fusion(f32[16,256,512]{2,1,0:T(8,128)S(1)} %fusion.6, f32[16,256]{1,0:T(8,128)S(1)} %broadcast_add_fusion, f32[512]{0:T(512)S(1)} %copy-done.2, f32[512,512]{1,0:T(8,128)S(1)} %copy-done), kind=kOutput, calls=%fused_computation.15 | convolution fusion | flops 12891193344 | bytes 17844224 | tf_op jit(solution)/shard_map/zj,cjab->czab/dot_general | solution.py:44
  508.1 10.3 %copy.17 = f32[1,512,16,256]{3,2,0,1:T(8,128)} copy(f32[1,512,16,256]{1,3,2,0:T(8,128)} %fusion.13) | data formatting | bytes 16777216 | tf_op jit(solution)/shard_map/zj,cjab->czab/transpose | solution.py:44
  518.3 5.0 all-to-all-start.1
  523.3 182.1 %all-to-all-done.1 = f32[1,512,16,256]{3,2,0,1:T(8,128)} async-done(((f32[1,512,16,256]{3,2,0,1:T(8,128)}), f32[1,512,16,256]{3,2,0,1:T(8,128)}, u32[]{:S(2)}, u32[]{:S(2)}) %all-to-all-start.1) | async-done | bytes 8388640 | tf_op jit(solution)/shard_map/all_to_all | solution.py:68
  705.5 4.4 copy.18
  709.8 0.0 copy-start.1
  709.8 15.4 %fusion.22 = f32[32,256,256]{2,1,0:T(8,128)S(1)} fusion(f32[32,256,256]{2,1,0:T(8,128)S(1)} %bitcast.52, f32[256]{0:T(256)S(1)} %fusion.34, pred[256]{0:T(512)(128)(4,1)S(1)} %iota_compare_fusion), kind=kOutput, calls=%fused_computation.25 | convolution fusion | flops 6443499520 | bytes 16778496 | tf_op jit(solution)/shard_map/jx,zjk->zxk/dot_general | solution.py:29
  725.3 17.9 %fusion.4 = f32[32,256,256]{2,1,0:T(8,128)} fusion(f32[32,256,256]{2,1,0:T(8,128)S(1)} %fusion.22, f32[256]{0:T(256)S(1)} %fusion.34, pred[256]{0:T(512)(128)(4,1)S(1)} %iota_compare_fusion), kind=kOutput, calls=%fused_computation.5 | convolution fusion | flops 6443499520 | bytes 16778496 | tf_op jit(solution)/shard_map/zxk,ky->zxy/dot_general | solution.py:30
  (7 shorter events, 0.1 us)
Async XLA Ops:
  6.5 463.7 %copy-start = (f32[512,512]{1,0:T(8,128)S(1)}, f32[512,512]{1,0:T(8,128)}, u32[]{:S(2)}) copy-start(f32[512,512]{1,0:T(8,128)} %param.8) | copy-start | bytes 3145732
  6.5 219.0 %all-reduce.2.cloned.1.call-start = ((), (), s32[]{:S(2)}) async-start(), calls=%async_computation.2 | async-start | bytes 16777216 | tf_op jit(solution)/shard_map/psum | solution.py:60
  271.7 188.9 %all-to-all-start = ((f32[1,32,256,256]{3,1,0,2:T(8,128)}), f32[1,32,256,256]{3,1,0,2:T(8,128)}, u32[]{:S(2)}, u32[]{:S(2)}) async-start(f32[1,32,256,256]{3,1,0,2:T(8,128)} %copy.13), calls=%async_computation | async-start | bytes 16777216 | tf_op jit(solution)/shard_map/all_to_all | solution.py:66
  470.2 21.4 %copy-start.2 = (f32[512]{0:T(512)S(1)}, f32[512]{0:T(512)}, u32[]{:S(2)}) copy-start(f32[512]{0:T(512)} %param.9) | copy-start | bytes 6148
  518.3 187.1 %all-to-all-start.1 = ((f32[1,512,16,256]{3,2,0,1:T(8,128)}), f32[1,512,16,256]{3,2,0,1:T(8,128)}, u32[]{:S(2)}, u32[]{:S(2)}) async-start(f32[1,512,16,256]{3,2,0,1:T(8,128)} %copy.17), calls=%async_computation.1 | async-start | bytes 16777216 | tf_op jit(solution)/shard_map/all_to_all | solution.py:68
  709.8 33.3 %copy-start.1 = (f32[512,512]{1,0:T(8,128)S(1)}, f32[512,512]{1,0:T(8,128)}, u32[]{:S(2)}) copy-start(f32[512,512]{1,0:T(8,128)} %param.8) | copy-start | bytes 3145732
Sparse Core Ops, SparseCore 0:
  26.5 198.9 all-reduce.1
where the time goes:
time: 759 us; the launch traced here: 750 us
  waiting for transfers between devices  563 us (74%)
  matrix products  107 us (14%)
  local copies, waits for them, and re-layouts  34.6 us (5%)
  other arithmetic  20 us (3%)
  between operations  13.9 us (2%)
  starting transfers between devices  11.5 us (2%)
    psum x1, waiting for transfers between devices, on_device(): density = lax.psum(partial_sum, 'kpt')  199 us
    all_to_all x1, waiting for transfers between devices, on_device(): lax.all_to_all(spectrum, 'grid', split_axis=2, concat_axis=1, tiled=True)  182 us
    all_to_all x1, waiting for transfers between devices, on_device(): lax.all_to_all(columns, 'grid', split_axis=1, concat_axis=2, tiled=True)  182 us
    dot_general x1, matrix products, forward_real(): return jnp.einsum('jx,zxk->zjk', table_x, along, precision=precise)[None]  23.2 us
    dot_general x1, matrix products, kernel_columns(): projected = jnp.einsum('zj,czab->cjab', z_rows, columns, precision=precise)  21.4 us
    reduce_sum x1, other arithmetic, on_device(): jnp.sum(factor[:, :, None, None, None, None] * values * values, axis=(0,...  18.9 us
    dot_general x1, matrix products, inverse_real(): return jnp.einsum('zxk,ky->zxy', half_done, scaled_y, precision=precise)  17.9 us
    dot_general x1, matrix products, kernel_columns(): jnp.einsum('zj,cjab->czab', z_rows, projected * factors[None], precision=...  16.4 us
  transfers between devices with their start and end apart: 3, of which 3 were waited for; matrix products, arithmetic and copies ran while one was open for 0% of the time, Pallas kernels for 0%

commit v1 on v0

--- a/solution.py
+++ b/solution.py
@@ -63,7 +63,17 @@
     kx_start = lax.axis_index("grid") * kx_count
     factors = scale_table(z_eigen, kx_start, kx_count, x_length, y_length)
     columns = kernel_columns(
-        z_basis, factors, lax.all_to_all(spectrum, "grid", split_axis=2, concat_axis=1, tiled=True)
+        z_basis,
+        factors,
+        jnp.concatenate(
+            lax.all_to_all(
+                jnp.stack(jnp.split(spectrum, lax.axis_size("grid"), axis=2)),
+                axis_name="grid",
+                split_axis=0,
+                concat_axis=0,
+            ),
+            axis=1,
+        ),
     )
     planes = lax.all_to_all(columns, "grid", split_axis=1, concat_axis=2, tiled=True)
     potential = inverse(planes)

time: 759 us -> 731 us (0.963)
  matrix products: 107 us -> 88.9 us
    dot_general x1, matrix products: 23.2 us -> 10.1 us  [forward_real(): return jnp.einsum('jx,zxk->zjk', table_x, along, precision=precise)[None]]
    unnamed x6 -> x21, local copies, waits for them, and re-layouts: 0.02 us -> 12.6 us
    broadcast_in_dim x1 -> x0, local copies, waits for them, and re-layouts: 10.3 us -> none  [forward_real(): return jnp.einsum('jx,zxk->zjk', table_x, along, precision=precise)[None]]
    all_to_all x2 -> x0, local copies, waits for them, and re-layouts: 9.66 us -> none  [on_device(): lax.all_to_all(spectrum, 'grid', split_axis=2, concat_axis=1, tiled=True)]
where the time goes in v1:
time: 731 us; the launch traced here: 726 us
  waiting for transfers between devices  563 us (77%)
  matrix products  88.9 us (12%)
  local copies, waits for them, and re-layouts  28.1 us (4%)
  other arithmetic  20 us (3%)
  between operations  13.7 us (2%)
  starting transfers between devices  12 us (2%)
    psum x1, waiting for transfers between devices, on_device(): density = lax.psum(partial_sum, 'kpt')  199 us
    all_to_all x1, waiting for transfers between devices, on_device(): lax.all_to_all(jnp.stack(jnp.split(spectrum, lax.axis_size('grid'), axis=...  182 us
    all_to_all x1, waiting for transfers between devices, on_device(): lax.all_to_all(columns, 'grid', split_axis=1, concat_axis=2, tiled=True)  182 us
    reduce_sum x1, other arithmetic, on_device(): jnp.sum(factor[:, :, None, None, None, None] * values * values, axis=(0,...  18.9 us
    dot_general x1, matrix products, inverse_real(): return jnp.einsum('zxk,ky->zxy', half_done, scaled_y, precision=precise)  17.9 us
    dot_general x1, matrix products, kernel_columns(): projected = jnp.einsum('zj,czab->cjab', z_rows, columns, precision=precise)  17.3 us
    dot_general x1, matrix products, kernel_columns(): jnp.einsum('zj,cjab->czab', z_rows, projected * factors[None], precision=...  16.4 us
    dot_general x1, matrix products, inverse_real(): jnp.einsum('jx,zjk->zxk', scaled_x, planes[0], precision=precise)  15.4 us
  transfers between devices with their start and end apart: 3, of which 3 were waited for; matrix products, arithmetic and copies ran while one was open for 0% of the time, Pallas kernels for 0%

profile of v1, /device:TPU:13, one launch (start us, length us, event | category | flops | bytes accessed | tf_op | source)
XLA Modules:
  0.0 725.9 jit_solution(302729634033786531)
XLA Ops:
  6.5 0.8 convert_multiply_fusion
  7.4 18.9 %fusion = f32[32,256,256]{2,1,0:T(8,128)} fusion(bf16[2,2,2,32,256,256]{5,4,3,2,1,0:T(8,128)(2,1)} %param.5, f32[2,2]{1,0:T(2,128)S(1)} %convert_multiply_fusion), kind=kLoop, calls=%fused_computation.1 | loop fusion | flops 65011712 | bytes 41943056 | tf_op jit(solution)/shard_map/reduce_sum | solution.py:54
  26.4 199.1 %all-reduce.2.cloned.1.call-done = f32[32,256,256]{2,1,0:T(8,128)} async-done(((f32[32,256,256]{2,1,0:T(8,128)}), f32[32,256,256]{2,1,0:T(8,128)}) %all-reduce.2.cloned.1.call-update) | async-done | bytes 8388624 | tf_op jit(solution)/shard_map/psum | solution.py:60
  225.5 11.9 %fusion.41 = f32[32,256,256]{2,1,0:T(8,128)S(1)} fusion(f32[32,256,256]{2,1,0:T(8,128)} %all-reduce.2.cloned.1.call-done, pred[256]{0:T(512)(128)(4,1)S(1)} %iota_compare_fusion), kind=kOutput, calls=%fused_computation.60 | convolution fusion | flops 6443433984 | bytes 16777472 | tf_op jit(solution)/shard_map/zxy,ky->zxk/dot_general | solution.py:23
  237.4 10.1 %convolution_bitcast_fusion = f32[1,32,256,256]{3,2,1,0:T(8,128)S(1)} fusion(f32[32,256,256]{2,1,0:T(8,128)S(1)} %fusion.41, pred[256]{0:T(512)(128)(4,1)S(1)} %iota_compare_fusion), kind=kOutput, calls=%fused_computation.14 | convolution fusion | flops 6443433984 | bytes 16777472 | tf_op jit(solution)/shard_map/jx,zxk->zjk/dot_general | solution.py:24
  247.5 0.8 fusion.33
  248.4 0.8 fusion.32
  249.2 0.8 fusion.31
  250.0 0.8 fusion.30
  250.9 0.8 fusion.29
  251.7 0.8 fusion.28
  252.6 0.8 fusion.27
  253.4 0.8 fusion.26
  254.2 0.8 fusion.25
  261.0 6.9 all-to-all-start
  268.0 182.0 %all-to-all-done = f32[16,1,32,16,256]{4,3,2,1,0:T(8,128)} async-done(((f32[16,1,32,16,256]{4,3,2,1,0:T(8,128)}), f32[16,1,32,16,256]{4,3,2,1,0:T(8,128)}, u32[]{:S(2)}, u32[]{:S(2)}) %all-to-all-start) | async-done | bytes 8388640 | tf_op jit(solution)/shard_map/all_to_all | solution.py:69
  450.0 17.3 %fusion.6 = f32[16,256,512]{2,1,0:T(8,128)S(1)} fusion(f32[512,16,256]{2,1,0:T(8,128)} %bitcast.20, f32[512,512]{1,0:T(8,128)S(1)} %copy-done), kind=kOutput, calls=%fused_computation.7 | convolution fusion | flops 12884901888 | bytes 17825792 | tf_op jit(solution)/shard_map/zj,czab->cjab/dot_general | solution.py:43
  467.4 16.4 %fusion.13 = f32[1,512,16,256]{1,3,2,0:T(8,128)} fusion(f32[16,256,512]{2,1,0:T(8,128)S(1)} %fusion.6, f32[16,256]{1,0:T(8,128)S(1)} %broadcast_add_fusion, f32[512]{0:T(512)S(1)} %copy-done.2, f32[512,512]{1,0:T(8,128)S(1)} %copy-done), kind=kOutput, calls=%fused_computation.15 | convolution fusion | flops 12891193344 | bytes 17844224 | tf_op jit(solution)/shard_map/zj,cjab->czab/dot_general | solution.py:44
  483.8 10.3 %copy.11 = f32[1,512,16,256]{3,2,0,1:T(8,128)} copy(f32[1,512,16,256]{1,3,2,0:T(8,128)} %fusion.13) | data formatting | bytes 16777216 | tf_op jit(solution)/shard_map/zj,cjab->czab/transpose | solution.py:44
  494.0 5.2 all-to-all-start.1
  499.2 181.9 %all-to-all-done.1 = f32[1,512,16,256]{3,2,0,1:T(8,128)} async-done(((f32[1,512,16,256]{3,2,0,1:T(8,128)}), f32[1,512,16,256]{3,2,0,1:T(8,128)}, u32[]{:S(2)}, u32[]{:S(2)}) %all-to-all-start.1) | async-done | bytes 8388640 | tf_op jit(solution)/shard_map/all_to_all | solution.py:78
  681.2 4.4 copy.12
  685.6 15.4 %fusion.38 = f32[32,256,256]{2,1,0:T(8,128)S(1)} fusion(f32[32,256,256]{2,1,0:T(8,128)S(1)} %bitcast.112, f32[256]{0:T(256)S(1)} %fusion.50, pred[256]{0:T(512)(128)(4,1)S(1)} %iota_compare_fusion), kind=kOutput, calls=%fused_computation.57 | convolution fusion | flops 6443499520 | bytes 16778496 | tf_op jit(solution)/shard_map/jx,zjk->zxk/dot_general | solution.py:29
  700.9 17.9 %fusion.4 = f32[32,256,256]{2,1,0:T(8,128)} fusion(f32[32,256,256]{2,1,0:T(8,128)S(1)} %fusion.38, f32[256]{0:T(256)S(1)} %fusion.50, pred[256]{0:T(512)(128)(4,1)S(1)} %iota_compare_fusion), kind=kOutput, calls=%fused_computation.5 | convolution fusion | flops 6443499520 | bytes 16778496 | tf_op jit(solution)/shard_map/zxk,ky->zxy/dot_general | solution.py:30
  (20 shorter events, 6.1 us)
Async XLA Ops:
  6.5 443.5 %copy-start = (f32[512,512]{1,0:T(8,128)S(1)}, f32[512,512]{1,0:T(8,128)}, u32[]{:S(2)}) copy-start(f32[512,512]{1,0:T(8,128)} %param.8) | copy-start | bytes 3145732
  6.5 219.0 %all-reduce.2.cloned.1.call-start = ((), (), s32[]{:S(2)}) async-start(), calls=%async_computation.2 | async-start | bytes 16777216 | tf_op jit(solution)/shard_map/psum | solution.py:60
  261.0 189.1 %all-to-all-start = ((f32[16,1,32,16,256]{4,3,2,1,0:T(8,128)}), f32[16,1,32,16,256]{4,3,2,1,0:T(8,128)}, u32[]{:S(2)}, u32[]{:S(2)}) async-start(f32[16,1,32,16,256]{4,3,2,1,0:T(8,128)} %fusion.18), calls=%async_computation | async-start | bytes 16777216 | tf_op jit(solution)/shard_map/all_to_all | solution.py:69
  450.0 17.4 %copy-start.2 = (f32[512]{0:T(512)S(1)}, f32[512]{0:T(512)}, u32[]{:S(2)}) copy-start(f32[512]{0:T(512)} %param.9) | copy-start | bytes 6148
  494.0 187.2 %all-to-all-start.1 = ((f32[1,512,16,256]{3,2,0,1:T(8,128)}), f32[1,512,16,256]{3,2,0,1:T(8,128)}, u32[]{:S(2)}, u32[]{:S(2)}) async-start(f32[1,512,16,256]{3,2,0,1:T(8,128)} %copy.11), calls=%async_computation.1 | async-start | bytes 16777216 | tf_op jit(solution)/shard_map/all_to_all | solution.py:78
  685.6 33.2 %copy-start.1 = (f32[512,512]{1,0:T(8,128)S(1)}, f32[512,512]{1,0:T(8,128)}, u32[]{:S(2)}) copy-start(f32[512,512]{1,0:T(8,128)} %param.8) | copy-start | bytes 3145732
Sparse Core Ops, SparseCore 0:
  26.5 198.9 all-reduce.1
